TPU v7x, 32 devices: a whole 2x2x4 slice. The times are simulated.
32 devices in a mesh: shard: 2 (over core), ctx: 4 (over y, x), tp: 4 (over z).
Axes of the slice: x: 2, y: 2, z: 4, core: 2. Of those that a mesh axis runs over, the one named last changes fastest.
Arguments:
- tokens: bfloat16 [2, 4096, 1024], P('shard', 'ctx'), may hold values from -6 to 6
- lengths: int32 [2], P('shard'), may hold values from 1024 to 4096, as said below
- routes: int32 [2, 4096, 1], P('shard', 'ctx'), may hold values from 0 to 7; in each aligned block of 1024 rows (0 to 1023, 1024 to 2047, ..., all dimensions but the last counted through in order) at most 384 rows name the same one
- priority: int32 [2, 4096], P('shard', 'ctx'), may hold values from 0 to 8191, as said below
- attn_gain: bfloat16 [1024], P(('shard', 'ctx')), may hold values from 0.5 to 1.5
- qkv_weight: bfloat16 [1024, 3, 1024], P(('shard', 'ctx'), None, 'tp'), may hold values from -0.1875 to 0.1875
- proj_weight: bfloat16 [1024, 1024], P('tp', ('shard', 'ctx')), may hold values from -2 to 2
- ffn_gain: bfloat16 [1024], P(('shard', 'ctx')), may hold values from 0.5 to 1.5
- mix_weight: bfloat16 [1024, 2], P(('shard', 'ctx')), may hold values from -0.1875 to 0.1875
- up_weight: bfloat16 [1024, 4096], P(('shard', 'ctx'), 'tp'), may hold values from -0.1875 to 0.1875
- down_weight: bfloat16 [4096, 1024], P('tp', ('shard', 'ctx')), may hold values from -0.09375 to 0.09375
- expert_up: bfloat16 [8, 1024, 4096], P(('shard', 'ctx'), None, 'tp'), may hold values from -0.1875 to 0.1875
- expert_down: bfloat16 [8, 4096, 1024], P(('shard', 'ctx'), 'tp'), may hold values from -0.09375 to 0.09375
- cotangent: bfloat16 [2, 4096, 1024], P('shard', 'ctx'), may hold values from -6 to 6
Outputs:
- layer_out: bfloat16 [2, 4096, 1024], P('shard', 'ctx')
- tokens_grad: bfloat16 [2, 4096, 1024], P('shard', 'ctx')
- attn_gain_grad: float32 [1024], P(('shard', 'ctx'))
- qkv_weight_grad: float32 [1024, 3, 1024], P(('shard', 'ctx'), None, 'tp')
- proj_weight_grad: float32 [1024, 1024], P('tp', ('shard', 'ctx'))
- ffn_gain_grad: float32 [1024], P(('shard', 'ctx'))
- mix_weight_grad: float32 [1024, 2], P(('shard', 'ctx'))
- up_weight_grad: float32 [1024, 4096], P(('shard', 'ctx'), 'tp')
- down_weight_grad: float32 [4096, 1024], P('tp', ('shard', 'ctx'))
- expert_up_grad: float32 [8, 1024, 4096], P(('shard', 'ctx'), None, 'tp')
- expert_down_grad: float32 [8, 4096, 1024], P(('shard', 'ctx'), 'tp')
Inputs may be any that keep to these rules, and one draw needn't show every extreme that they name: `lengths`: padding positions are those at or past a slot's length; some slot has exactly 4096 live positions. `routes`: in the rows of one device (one slot's 1024 positions on one index of ctx), at most 384 positions name the same expert, and exactly 384 do for some expert on some device. `priority`: each value 0 to 8191 occurs at exactly one position of all slots.
All inputs are finite; a program needn't handle non-finite values.
Results may differ from a plain program's by a relative error of at most 0.024.
Values may be sent and summed in bfloat16 or wider, within the bound.
A program may use at most 192 MiB of HBM per device.

v0:
```python
import jax
import jax.numpy as jnp
from jax import lax
from jax.sharding import PartitionSpec as P

HD = 64
CAP = 1152
empty_mark = 1 << 30
norm_eps = 1e-05
masked_score = -1e30


def gelu_tanh(values):
    return jax.nn.gelu(values, approximate=True)


def norm_forward(values, gain_vec):
    average = jnp.mean(values, axis=-1, keepdims=True)
    centred = values - average
    spread = jnp.mean(centred * centred, axis=-1, keepdims=True)
    inverse = lax.rsqrt(spread + norm_eps)
    unit_rows = centred * inverse
    return (unit_rows * gain_vec, unit_rows, inverse)


def norm_backward(upstream, gain_vec, unit_rows, inverse):
    shaped = upstream * gain_vec
    first_term = jnp.mean(shaped, axis=-1, keepdims=True)
    second_term = jnp.mean(shaped * unit_rows, axis=-1, keepdims=True)
    return (
        inverse * (shaped - first_term - unit_rows * second_term),
        jnp.sum(upstream * unit_rows, axis=0),
    )


def local(
    tokens,
    lengths,
    routes,
    priority,
    attn_gain,
    qkv_weight,
    proj_weight,
    ffn_gain,
    mix_weight,
    up_weight,
    down_weight,
    expert_up,
    expert_down,
    cotangent,
):
    seq_dev = tokens.shape[1]
    model_width = tokens.shape[2]
    full_len = seq_dev * lax.axis_size("ctx")
    positions = lax.axis_index("ctx") * seq_dev + jnp.arange(seq_dev, dtype=jnp.int32)
    live_mask = positions < lengths[0]
    live_rows = live_mask.astype(jnp.float32)[:, None]
    inputs = tokens[0].astype(jnp.float32)
    gain_one, qkv_full, proj_full, gain_two, mix_full, up_full, down_full = (
        lax.all_gather(attn_gain, ("shard", "ctx"), axis=0, tiled=True),
        lax.all_gather(qkv_weight, ("shard", "ctx"), axis=0, tiled=True),
        lax.all_gather(proj_weight, ("shard", "ctx"), axis=1, tiled=True),
        lax.all_gather(ffn_gain, ("shard", "ctx"), axis=0, tiled=True),
        lax.all_gather(mix_weight, ("shard", "ctx"), axis=0, tiled=True),
        lax.all_gather(up_weight, ("shard", "ctx"), axis=0, tiled=True),
        lax.all_gather(down_weight, ("shard", "ctx"), axis=1, tiled=True),
    )
    gain_one = gain_one.astype(jnp.float32)
    gain_two = gain_two.astype(jnp.float32)
    local_heads = qkv_full.shape[2] // HD
    score_scale = HD ** (-0.5)
    normed, unit_one, inverse_one = norm_forward(inputs, gain_one)
    normed_low = normed.astype(jnp.bfloat16)
    projected = jnp.einsum(
        "td,dcf->tcf", normed_low, qkv_full, preferred_element_type=jnp.float32
    ).astype(jnp.bfloat16)
    queries = projected[:, 0].reshape(seq_dev, local_heads, HD)
    keys_all, values_all = (
        lax.all_gather(projected[:, 1], "ctx", axis=0, tiled=True),
        lax.all_gather(projected[:, 2], "ctx", axis=0, tiled=True),
    )
    key_block = min(full_len, 1024)
    block_count = full_len // key_block
    key_blocks = keys_all.reshape(block_count, key_block, local_heads, HD)
    value_blocks = values_all.reshape(block_count, key_block, local_heads, HD)
    key_places = jnp.arange(full_len, dtype=jnp.int32).reshape(block_count, key_block)

    def allowed(places):
        return ((places[None, :] <= positions[:, None]) & (places[None, :] < lengths[0]))[None]

    def forward_step(state_now, pieces):
        running_max, running_sum, weighted = state_now
        key_rows, value_rows, places = pieces
        visible = allowed(places)
        scores = (
            jnp.einsum("qhd,khd->hqk", queries, key_rows, preferred_element_type=jnp.float32)
            * score_scale
        )
        scores = jnp.where(visible, scores, masked_score)
        new_max = jnp.maximum(running_max, jnp.max(scores, axis=-1))
        weights = jnp.where(visible, jnp.exp(scores - new_max[..., None]), 0.0)
        shrink = jnp.exp(running_max - new_max)
        running_sum = running_sum * shrink + jnp.sum(weights, axis=-1)
        weighted = weighted * shrink[..., None] + jnp.einsum(
            "hqk,khd->hqd",
            weights.astype(jnp.bfloat16),
            value_rows,
            preferred_element_type=jnp.float32,
        )
        return ((new_max, running_sum, weighted), None)

    start_state = (
        jnp.full((local_heads, seq_dev), masked_score, jnp.float32),
        jnp.zeros((local_heads, seq_dev), jnp.float32),
        jnp.zeros((local_heads, seq_dev, HD), jnp.float32),
    )
    (running_max, running_sum, weighted), _ = lax.scan(
        forward_step, start_state, (key_blocks, value_blocks, key_places)
    )
    log_total = running_max + jnp.log(running_sum)
    heads_out = weighted / running_sum[..., None]
    attended_low = jnp.transpose(heads_out, (1, 0, 2)).reshape(seq_dev, -1).astype(jnp.bfloat16)
    branch_part = jnp.dot(attended_low, proj_full, preferred_element_type=jnp.float32)
    branch = lax.psum(branch_part.astype(jnp.bfloat16), "tp").astype(jnp.float32)
    middle = inputs + branch
    normed2, unit_two, inverse_two = norm_forward(middle, gain_two)
    normed2_low = normed2.astype(jnp.bfloat16)
    mixing = jax.nn.softmax(
        jnp.dot(normed2_low, mix_full, preferred_element_type=jnp.float32), axis=-1
    )
    upper_pre = jnp.dot(normed2_low, up_full, preferred_element_type=jnp.float32)
    hidden_low = gelu_tanh(upper_pre).astype(jnp.bfloat16)
    dense_part = jnp.dot(hidden_low, down_full, preferred_element_type=jnp.float32)
    experts_total = lax.axis_size(("shard", "ctx"))
    slot_cap = max(4, 3 * seq_dev // experts_total)
    chosen = routes[0, :, 0]
    onehot = (chosen[:, None] == jnp.arange(experts_total, dtype=jnp.int32)[None, :]).astype(
        jnp.int32
    )
    slot_pos = jnp.sum(jnp.cumsum(onehot, axis=0) * onehot, axis=1) - 1
    target = jnp.where(live_mask, chosen * slot_cap + slot_pos, experts_total * slot_cap)

    def pack_rows(token_rows):
        buffer = jnp.zeros((experts_total * slot_cap, model_width), token_rows.dtype)
        return (
            buffer.at[target]
            .set(token_rows, mode="drop")
            .reshape(experts_total, slot_cap, model_width)
        )

    send_order = (
        jnp.full((experts_total * slot_cap,), empty_mark, jnp.int32)
        .at[target]
        .set(priority[0], mode="drop")
    )
    recv_rows, recv_order = (
        lax.all_to_all(
            pack_rows(normed2_low), ("shard", "ctx"), split_axis=0, concat_axis=0, tiled=True
        ),
        lax.all_to_all(
            send_order.reshape(experts_total, slot_cap),
            ("shard", "ctx"),
            split_axis=0,
            concat_axis=0,
            tiled=True,
        ),
    )
    flat_order = recv_order.reshape(-1)
    ranking = jnp.argsort(flat_order)[:CAP]
    taken_mask = (flat_order[ranking] < empty_mark).astype(jnp.float32)[:, None]
    expert_in = recv_rows.reshape(-1, model_width)[ranking]
    own_up = expert_up[0]
    own_down = expert_down[0]
    expert_pre = jnp.dot(expert_in, own_up, preferred_element_type=jnp.float32)
    expert_hidden = gelu_tanh(expert_pre).astype(jnp.bfloat16)
    expert_part = jnp.dot(expert_hidden, own_down, preferred_element_type=jnp.float32) * taken_mask

    def unfold_rows(slot_rows):
        buffer = jnp.zeros((experts_total * slot_cap, model_width), jnp.float32)
        return buffer.at[ranking].set(slot_rows).reshape(experts_total, slot_cap, model_width)

    full_index = jnp.where(live_mask, chosen * slot_cap + slot_pos, 0)
    returned_rows = lax.all_to_all(
        unfold_rows(expert_part).astype(jnp.bfloat16),
        ("shard", "ctx"),
        split_axis=0,
        concat_axis=0,
        tiled=True,
    ).astype(jnp.float32)
    expert_tok = returned_rows.reshape(-1, model_width)[full_index] * live_rows
    mixed_part = mixing[:, 0:1] * dense_part + mixing[:, 1:2] * expert_tok
    mixed = lax.psum(mixed_part.astype(jnp.bfloat16), "tp").astype(jnp.float32)
    layer_out = ((middle + mixed) * live_rows).astype(jnp.bfloat16)[None]
    out_grad = cotangent[0].astype(jnp.float32) * live_rows
    dense_grad = (mixing[:, 0:1] * out_grad).astype(jnp.bfloat16)
    expert_grad = (mixing[:, 1:2] * out_grad).astype(jnp.bfloat16)
    dots_part = jnp.stack(
        [jnp.sum(out_grad * dense_part, axis=-1), jnp.sum(out_grad * expert_tok, axis=-1)], axis=-1
    )
    down_grad = jnp.einsum("tf,td->fd", hidden_low, dense_grad, preferred_element_type=jnp.float32)
    hidden_grad = jnp.einsum("td,fd->tf", dense_grad, down_full, preferred_element_type=jnp.float32)
    _, gelu_pull = jax.vjp(gelu_tanh, upper_pre)
    upper_grad = gelu_pull(hidden_grad)[0].astype(jnp.bfloat16)
    up_grad = jnp.einsum("td,tf->df", normed2_low, upper_grad, preferred_element_type=jnp.float32)
    normed2_part = jnp.einsum("tf,df->td", upper_grad, up_full, preferred_element_type=jnp.float32)
    recv_grad = lax.all_to_all(
        pack_rows(expert_grad), ("shard", "ctx"), split_axis=0, concat_axis=0, tiled=True
    )
    grad_in = recv_grad.reshape(-1, model_width)[ranking]
    own_down_grad = jnp.einsum(
        "cf,cd->fd", expert_hidden, grad_in, preferred_element_type=jnp.float32
    )
    ehidden_grad = jnp.einsum("cd,fd->cf", grad_in, own_down, preferred_element_type=jnp.float32)
    _, expert_pull = jax.vjp(gelu_tanh, expert_pre)
    epre_grad = expert_pull(ehidden_grad)[0].astype(jnp.bfloat16)
    own_up_grad = jnp.einsum("cd,cf->df", expert_in, epre_grad, preferred_element_type=jnp.float32)
    expert_in_grad = jnp.einsum("cf,df->cd", epre_grad, own_up, preferred_element_type=jnp.float32)
    sent_back = lax.all_to_all(
        unfold_rows(expert_in_grad).astype(jnp.bfloat16),
        ("shard", "ctx"),
        split_axis=0,
        concat_axis=0,
        tiled=True,
    ).astype(jnp.float32)
    expert_tok_grad = sent_back.reshape(-1, model_width)[full_index] * live_rows
    normed2_grad, branch_dots = (
        lax.psum((normed2_part + expert_tok_grad).astype(jnp.bfloat16), "tp").astype(jnp.float32),
        lax.psum(dots_part.astype(jnp.bfloat16), "tp").astype(jnp.float32),
    )
    logit_grad = mixing * (branch_dots - jnp.sum(mixing * branch_dots, axis=-1, keepdims=True))
    mix_grad = jnp.dot(
        normed2_low.astype(jnp.float32).T, logit_grad, precision=lax.Precision.HIGHEST
    )
    normed2_grad = normed2_grad + jnp.dot(
        logit_grad, mix_full.astype(jnp.float32).T, precision=lax.Precision.HIGHEST
    )
    middle_norm_grad, gain_two_grad = norm_backward(normed2_grad, gain_two, unit_two, inverse_two)
    middle_grad = out_grad + middle_norm_grad
    branch_grad = middle_grad.astype(jnp.bfloat16)
    proj_grad = jnp.einsum(
        "tf,td->fd", attended_low, branch_grad, preferred_element_type=jnp.float32
    )
    attended_grad = jnp.einsum(
        "td,fd->tf", branch_grad, proj_full, preferred_element_type=jnp.float32
    ).astype(jnp.bfloat16)
    grad_heads = attended_grad.reshape(seq_dev, local_heads, HD)
    row_delta = jnp.sum(
        jnp.transpose(grad_heads, (1, 0, 2)).astype(jnp.float32) * heads_out, axis=-1
    )

    def backward_step(query_grad, pieces):
        key_rows, value_rows, places = pieces
        visible = allowed(places)
        scores = (
            jnp.einsum("qhd,khd->hqk", queries, key_rows, preferred_element_type=jnp.float32)
            * score_scale
        )
        probs = jnp.where(visible, jnp.exp(scores - log_total[..., None]), 0.0)
        prob_grad = jnp.einsum(
            "qhd,khd->hqk", grad_heads, value_rows, preferred_element_type=jnp.float32
        )
        score_grad = (probs * (prob_grad - row_delta[..., None])).astype(jnp.bfloat16)
        query_grad = query_grad + jnp.einsum(
            "hqk,khd->qhd", score_grad, key_rows, preferred_element_type=jnp.float32
        )
        key_grad = jnp.einsum(
            "hqk,qhd->khd", score_grad, queries, preferred_element_type=jnp.float32
        )
        value_grad = jnp.einsum(
            "hqk,qhd->khd",
            probs.astype(jnp.bfloat16),
            grad_heads,
            preferred_element_type=jnp.float32,
        )
        return (query_grad, (key_grad, value_grad))

    query_grad, (key_grad_blocks, value_grad_blocks) = lax.scan(
        backward_step,
        jnp.zeros((seq_dev, local_heads, HD), jnp.float32),
        (key_blocks, value_blocks, key_places),
    )
    key_grad_all = key_grad_blocks.reshape(full_len, -1) * score_scale
    value_grad_all = value_grad_blocks.reshape(full_len, -1)
    key_grad_own, value_grad_own = (
        lax.psum_scatter(
            key_grad_all.astype(jnp.bfloat16), "ctx", scatter_dimension=0, tiled=True
        ).astype(jnp.float32),
        lax.psum_scatter(
            value_grad_all.astype(jnp.bfloat16), "ctx", scatter_dimension=0, tiled=True
        ).astype(jnp.float32),
    )
    qkv_grad = jnp.stack(
        [(query_grad * score_scale).reshape(seq_dev, -1), key_grad_own, value_grad_own], axis=1
    ).astype(jnp.bfloat16)
    qkv_grad_full = jnp.einsum(
        "td,tcf->dcf", normed_low, qkv_grad, preferred_element_type=jnp.float32
    )
    normed_part = jnp.einsum("tcf,dcf->td", qkv_grad, qkv_full, preferred_element_type=jnp.float32)
    normed_grad = lax.psum(normed_part.astype(jnp.bfloat16), "tp").astype(jnp.float32)
    input_norm_grad, gain_one_grad = norm_backward(normed_grad, gain_one, unit_one, inverse_one)
    tokens_grad = (middle_grad + input_norm_grad).astype(jnp.bfloat16)[None]
    shares = (
        lax.psum_scatter(gain_one_grad, ("shard", "ctx"), scatter_dimension=0, tiled=True),
        lax.psum_scatter(qkv_grad_full, ("shard", "ctx"), scatter_dimension=0, tiled=True),
        lax.psum_scatter(proj_grad, ("shard", "ctx"), scatter_dimension=1, tiled=True),
        lax.psum_scatter(gain_two_grad, ("shard", "ctx"), scatter_dimension=0, tiled=True),
        lax.psum_scatter(mix_grad, ("shard", "ctx"), scatter_dimension=0, tiled=True),
        lax.psum_scatter(up_grad, ("shard", "ctx"), scatter_dimension=0, tiled=True),
        lax.psum_scatter(down_grad, ("shard", "ctx"), scatter_dimension=1, tiled=True),
    )
    return (
        layer_out,
        tokens_grad,
        shares[0],
        shares[1],
        shares[2],
        shares[3],
        shares[4],
        shares[5],
        shares[6],
        own_up_grad[None],
        own_down_grad[None],
    )


def solution(mesh):
    placed = (
        P("shard", "ctx", None),
        P("shard"),
        P("shard", "ctx", None),
        P("shard", "ctx"),
        P(("shard", "ctx")),
        P(("shard", "ctx"), None, "tp"),
        P("tp", ("shard", "ctx")),
        P(("shard", "ctx")),
        P(("shard", "ctx"), None),
        P(("shard", "ctx"), "tp"),
        P("tp", ("shard", "ctx")),
        P(("shard", "ctx"), None, "tp"),
        P(("shard", "ctx"), "tp", None),
        P("shard", "ctx", None),
    )
    return jax.shard_map(
        local,
        mesh=mesh,
        in_specs=placed,
        out_specs=(
            P("shard", "ctx", None),
            P("shard", "ctx", None),
            P(("shard", "ctx")),
            P(("shard", "ctx"), None, "tp"),
            P("tp", ("shard", "ctx")),
            P(("shard", "ctx")),
            P(("shard", "ctx"), None),
            P(("shard", "ctx"), "tp"),
            P("tp", ("shard", "ctx")),
            P(("shard", "ctx"), None, "tp"),
            P(("shard", "ctx"), "tp", None),
        ),
        check_vma=False,
    )
```

profile of v0, /device:TPU:0, one launch (start us, length us, event | category | flops | bytes accessed | tf_op | source)
XLA Modules:
  0.0 1538.6 jit_solution(16928028134594946048)
XLA Ops:
  9.2 15.0 all-gather.2
  28.5 10.5 all-gather.10.cloned.1.call-done
  45.0 24.4 %all_gather.31 = bf16[256,1024]{1,0:T(8,128)(2,1)S(1)} all-gather(bf16[256,128]{1,0:T(8,128)(2,1)S(1)} %copy-done.32), channel_id=1, replica_groups=mesh['shard'=2,'ctx'=4,'tp'=4] {'shard','ctx'}, dimensions={1}, use_global_device_ids=true | all-gather | bytes 589824 | tf_op jit(solution)/shard_map/all_gather | solution.py:62
  69.4 13.8 all-gather.18.cloned.1.call-done
  91.3 29.6 %all-gather.16.cloned.1.call-done = bf16[4096,1,256]{0,2,1:T(8,128)(2,1)} async-done(((bf16[1024,1,256]{0,2,1:T(8,128)(2,1)}), bf16[4096,1,256]{0,2,1:T(8,128)(2,1)}) %all-gather.16.cloned.1.call-update) | async-done | bytes 2097168 | tf_op jit(solution)/shard_map/all_gather | solution.py:79
  128.9 67.9 %while.30 = (s32[]{:T(128)}, f32[4,1024]{1,0:T(4,128)S(1)}, f32[4,1024]{1,0:T(4,128)S(1)}, f32[4,1024,64]{1,2,0:T(8,128)}, s32[4,1024]{1,0:T(4,128)S(1)}, /*inde...) while((s32[]{:T(128)}, f32[4,1024]{1,0:T(4,128)S(1)}, ...), condition=%wide.region_5.6_spmd.clone, body=%wide.region_2.5_spmd.clone.sunk | while | flops 1131173888 | bytes 66869456 | solution.py:117
  213.3 14.5 all-gather.3
  227.8 59.8 %all-reduce.8.cloned.1.call-done = bf16[1024,1024]{1,0:T(8,128)(2,1)} async-done(((bf16[1024,1024]{1,0:T(8,128)(2,1)}), bf16[1024,1024]{1,0:T(8,128)(2,1)}) %all-reduce.8.cloned.1.call-update) | async-done | bytes 2097168 | tf_op jit(solution)/shard_map/psum | solution.py:124
  294.8 9.8 scatter_custom_fusion.1
  322.2 66.5 %all-to-all-done.1 = bf16[8,384,1024]{2,1,0:T(8,128)(2,1)} async-done(((bf16[8,384,1024]{2,1,0:T(8,128)(2,1)}), bf16[8,384,1024]{2,1,0:T(8,128)(2,1)}, u32[]{:S(2)}, u32[]{:S(2)}) %all-to-all-start.1) | async-done | bytes 6291488 | tf_op jit(solution)/shard_map/all_to_all | solution.py:157
  388.8 10.2 gather_fusion
  410.7 14.5 scatter_custom_fusion.2
  438.9 86.6 %all_gather.33 = bf16[1024,2]{0,1:T(2,128)(2,1)S(1)} all-gather(bf16[128,2]{0,1:T(2,128)(2,1)S(1)} %copy-done.54), channel_id=1, replica_groups=mesh['shard'=2,'ctx'=4,'tp'=4] {'shard','ctx'}, dimensions={0}, use_global_device_ids=true | all-gather | bytes 4608 | tf_op jit(solution)/shard_map/all_gather | solution.py:64
  543.2 10.9 gather_fusion.2
  554.1 9.6 fusion.91
  563.7 10.0 psum.38
  573.8 10.1 scatter_custom_fusion.3
  583.9 76.7 %all_to_all.29 = bf16[8,384,1024]{2,1,0:T(8,128)(2,1)} all-to-all(bf16[8,384,1024]{2,1,0:T(8,128)(2,1)} %bitcast.322), channel_id=1, replica_groups=mesh['shard'=2,'ctx'=4,'tp'=4] {'shard','ctx'}, dimensions={0} | all-to-all | bytes 12582912 | tf_op jit(solution)/shard_map/all_to_all | solution.py:206
  660.6 10.2 gather_fusion.3
  684.5 14.3 scatter_custom_fusion.4
  720.6 62.3 %all-to-all-done.4 = bf16[8,384,1024]{2,1,0:T(8,128)(2,1)} async-done(((bf16[8,384,1024]{2,1,0:T(8,128)(2,1)}), bf16[8,384,1024]{2,1,0:T(8,128)(2,1)}, u32[]{:S(2)}, u32[]{:S(2)}) %all-to-all-start.4) | async-done | bytes 6291488 | tf_op jit(solution)/shard_map/all_to_all | solution.py:218
  791.8 11.0 gather_fusion.4
  810.2 83.1 %all-reduce.10.cloned.1.call-done = bf16[1024,1024]{1,0:T(8,128)(2,1)} async-done(((bf16[1024,1024]{1,0:T(8,128)(2,1)}), bf16[1024,1024]{1,0:T(8,128)(2,1)}) %all-reduce.10.cloned.1.call-update) | async-done | bytes 2097168 | tf_op jit(solution)/shard_map/psum | solution.py:227
  907.0 144.0 %while.31 = (s32[]{:T(128)}, f32[1024,4,64]{0,2,1:T(8,128)S(1)}, f32[4,1024,4,64]{1,3,2,0:T(8,128)}, bf16[4,1024,4,64]{1,3,2,0:T(8,128)(2,1)}, bf16[4,1024,4,64]...) while((s32[]{:T(128)}, f32[1024,4,64]{0,2,1:T(8,128)S(1)}, ...), condition=%wide.region_30.31_spmd.clone, body=%wide.region_29.30_spmd.clone.sunk | while | flops 2728921088 | bytes 86579392 | solution.py:277
  1085.2 14.1 reduce-scatter.12.cloned.1.call-done
  1099.3 38.2 %reduce-scatter.10.cloned.1.call-done = bf16[1024,256]{1,0:T(8,128)(2,1)} async-done(((bf16[4096,256]{1,0:T(8,128)(2,1)}), bf16[1024,256]{1,0:T(8,128)(2,1)}) %reduce-scatter.10.cloned.1.call-update) | async-done | bytes 524304 | tf_op jit(solution)/shard_map/reduce_scatter | solution.py:285
  1189.0 144.2 %all-reduce.12.cloned.1.call-done = (bf16[1024,1024]{1,0:T(8,128)(2,1)}, bf16[1024,1024]{1,0:T(8,128)(2,1)}) async-done(((bf16[1024,1024]{1,0:T(8,128)(2,1)}, bf16[1024,1024]{1,0:T(8,128)(2,1)}), (bf16[1024,1024]{1,0:T(8,128)(2,1)}, bf16[1024,1024]{1,0:T(8,128)(2,1)})) %all-reduce.12.cloned.1.call-update) | async-done | bytes 4194320 | tf_op jit(solution)/shard_map/psum | solution.py:192
  1336.7 14.7 all-reduce.2
  1359.8 27.3 %reduce-scatter.20.cloned.1.call-done = f32[1024,128]{1,0:T(8,128)} async-done(((f32[1024,1024]{1,0:T(8,128)}), f32[1024,128]{1,0:T(8,128)}) %reduce-scatter.20.cloned.1.call-update) | async-done | bytes 524304 | tf_op jit(solution)/shard_map/reduce_scatter | solution.py:309
  1387.0 55.1 %reduce-scatter.18.cloned.1.call-done = f32[128,1024]{1,0:T(8,128)} async-done(((f32[1024,1024]{1,0:T(8,128)}), f32[128,1024]{1,0:T(8,128)}) %reduce-scatter.18.cloned.1.call-update) | async-done | bytes 524304 | tf_op jit(solution)/shard_map/reduce_scatter | solution.py:308
  1442.2 39.6 %reduce-scatter.16.cloned.1.call-done = f32[256,128]{1,0:T(8,128)} async-done(((f32[256,1024]{1,0:T(8,128)}), f32[256,128]{1,0:T(8,128)}) %reduce-scatter.16.cloned.1.call-update) | async-done | bytes 131088 | tf_op jit(solution)/shard_map/reduce_scatter | solution.py:305
  1481.8 49.9 %reduce-scatter.14.cloned.1.call-done = f32[128,3,256]{2,0,1:T(8,128)} async-done(((f32[1024,3,256]{2,0,1:T(8,128)}), f32[128,3,256]{2,0,1:T(8,128)}) %reduce-scatter.14.cloned.1.call-update) | async-done | bytes 393232 | tf_op jit(solution)/shard_map/reduce_scatter | solution.py:304
  (333 shorter events, 485.1 us)
Async XLA Ops:
  7.2 398.9 %copy-start = (bf16[1,1024,1024]{2,1,0:T(8,128)(2,1)S(1)}, bf16[1,1024,1024]{2,1,0:T(8,128)(2,1)}, u32[]{:S(2)}) copy-start(bf16[1,1024,1024]{2,1,0:T(8,128)(2,1)} %param.30) | copy-start | bytes 6291460
  7.2 31.8 %all-gather.10.cloned.1.call-start = ((), (), s32[]{:S(2)}) async-start(), calls=%async_computation.12 | async-start | bytes 1769472 | tf_op jit(solution)/shard_map/all_gather | solution.py:61
  9.1 74.1 %all-gather.18.cloned.1.call-start = ((), (), s32[]{:S(2)}) async-start(), calls=%async_computation.24 | async-start | bytes 2621440 | tf_op jit(solution)/shard_map/all_gather | solution.py:80
  44.2 76.8 %all-gather.16.cloned.1.call-start = ((), (), s32[]{:S(2)}) async-start(), calls=%async_computation.23 | async-start | bytes 2621440 | tf_op jit(solution)/shard_map/all_gather | solution.py:79
  44.9 242.7 %all-reduce.8.cloned.1.call-start = ((), (), s32[]{:S(2)}) async-start(), calls=%async_computation.13 | async-start | bytes 4194304 | tf_op jit(solution)/shard_map/psum | solution.py:124
  69.4 129.0 %copy-start.14 = (bf16[256,1024]{1,0:T(8,128)(2,1)}, bf16[256,1024]{1,0:T(8,128)(2,1)S(1)}, u32[]{:S(2)}) copy-start(bf16[256,1024]{1,0:T(8,128)(2,1)S(1)} %all_gather.31) | copy-start | bytes 1572868
  196.9 93.8 %copy-start.23 = (f32[4,1024]{1,0:T(4,128)}, f32[4,1024]{1,0:T(4,128)S(1)}, u32[]{:S(2)}) copy-start(f32[4,1024]{1,0:T(4,128)S(1)} %get-tuple-element.138) | copy-start | bytes 49156
  196.9 93.8 %copy-start.25 = (f32[4,1024]{1,0:T(4,128)}, f32[4,1024]{1,0:T(4,128)S(1)}, u32[]{:S(2)}) copy-start(f32[4,1024]{1,0:T(4,128)S(1)} %get-tuple-element.136) | copy-start | bytes 49156
  196.9 93.8 %copy-start.27 = (s32[4,1024]{1,0:T(4,128)}, s32[4,1024]{1,0:T(4,128)S(1)}, u32[]{:S(2)}) copy-start(s32[4,1024]{1,0:T(4,128)S(1)} %get-tuple-element.679) | copy-start | bytes 49156
  209.9 94.7 %all-to-all-start = ((s32[8,1,384]{2,1,0:T(1,128)}), s32[8,1,384]{2,1,0:T(1,128)S(1)}, u32[]{:S(2)}, u32[]{:S(2)}) async-start(s32[8,1,384]{2,1,0:T(1,128)} %bitcast.19), calls=%async_computation | async-start | bytes 24576 | tf_op jit(solution)/shard_map/all_to_all | solution.py:160
  304.6 84.1 %all-to-all-start.1 = ((bf16[8,384,1024]{2,1,0:T(8,128)(2,1)}), bf16[8,384,1024]{2,1,0:T(8,128)(2,1)}, u32[]{:S(2)}, u32[]{:S(2)}) async-start(bf16[8,384,1024]{2,1,0:T(8,128)(2,1)} %bitcast.321), calls=%async_computation.1 | async-start | bytes 12582912 | tf_op jit(solution)/shard_map/all_to_all | solution.py:157
  309.4 218.4 %all-gather.12.cloned.1.call-start = ((), (), s32[]{:S(2)}) async-start(), calls=%async_computation.14 | async-start | bytes 2359296 | tf_op jit(solution)/shard_map/all_gather | solution.py:65
  433.3 101.0 %all-to-all-start.2 = ((bf16[8,384,1024]{2,1,0:T(8,128)(2,1)}), bf16[8,384,1024]{2,1,0:T(8,128)(2,1)}, u32[]{:S(2)}, u32[]{:S(2)}) async-start(bf16[8,384,1024]{2,1,0:T(8,128)(2,1)} %bitcast.323), calls=%async_computation.2 | async-start | bytes 12582912 | tf_op jit(solution)/shard_map/all_to_all | solution.py:183
  438.3 115.8 %all-gather.14.cloned.1.call-start = ((), (), s32[]{:S(2)}) async-start(), calls=%async_computation.15 | async-start | bytes 2359296 | tf_op jit(solution)/shard_map/all_gather | solution.py:66
  525.4 374.7 %copy-start.30 = (f32[1024]{0:T(1024)}, f32[1024]{0:T(1024)S(1)}, u32[]{:S(2)}) copy-start(f32[1024]{0:T(1024)S(1)} %fusion.129) | copy-start | bytes 12292
  573.7 319.6 %copy-start.37 = (bf16[1024,2]{0,1:T(2,128)(2,1)}, bf16[1024,2]{0,1:T(2,128)(2,1)S(1)}, u32[]{:S(2)}) copy-start(bf16[1024,2]{0,1:T(2,128)(2,1)S(1)} %psum.38) | copy-start | bytes 12292
  573.8 319.5 %copy-start.28 = (f32[1024,2]{0,1:T(2,128)}, f32[1024,2]{0,1:T(2,128)S(1)}, u32[]{:S(2)}) copy-start(f32[1024,2]{0,1:T(2,128)S(1)} %get-tuple-element.357) | copy-start | bytes 24580
  573.8 319.5 %copy-start.50 = (f32[1024]{0:T(1024)}, f32[1024]{0:T(1024)S(1)}, u32[]{:S(2)}) copy-start(f32[1024]{0:T(1024)S(1)} %get-tuple-element.356) | copy-start | bytes 12292
  573.8 326.3 %copy-start.48 = (f32[1024,1]{0,1:T(1,128)}, f32[1024,1]{0,1:T(1,128)S(1)}, u32[]{:S(2)}) copy-start(f32[1024,1]{0,1:T(1,128)S(1)} %get-tuple-element.365) | copy-start | bytes 12292
  707.0 75.9 %all-to-all-start.4 = ((bf16[8,384,1024]{2,1,0:T(8,128)(2,1)}), bf16[8,384,1024]{2,1,0:T(8,128)(2,1)}, u32[]{:S(2)}, u32[]{:S(2)}) async-start(bf16[8,384,1024]{2,1,0:T(8,128)(2,1)} %bitcast.324), calls=%async_computation.4 | async-start | bytes 12582912 | tf_op jit(solution)/shard_map/all_to_all | solution.py:218
  711.9 181.4 %all-reduce.10.cloned.1.call-start = ((), (), s32[]{:S(2)}) async-start(), calls=%async_computation.16 | async-start | bytes 4194304 | tf_op jit(solution)/shard_map/psum | solution.py:227
  802.8 90.6 %copy-start.45 = (f32[8,1,128]{2,1,0:T(1,128)S(1)}, f32[8,1,128]{2,1,0:T(1,128)}, u32[]{:S(2)}) copy-start(f32[8,1,128]{2,1,0:T(1,128)} %copy-done.44) | copy-start | bytes 12292
  810.1 289.2 %reduce-scatter.12.cloned.1.call-start = ((), (), s32[]{:S(2)}) async-start(), calls=%async_computation.18 | async-start | bytes 2621440 | tf_op jit(solution)/shard_map/reduce_scatter | solution.py:288
  1064.9 72.6 %reduce-scatter.10.cloned.1.call-start = ((), (), s32[]{:S(2)}) async-start(), calls=%async_computation.17 | async-start | bytes 2621440 | tf_op jit(solution)/shard_map/reduce_scatter | solution.py:285
  1079.8 95.3 %reduce-scatter.22.cloned.1.call-start = ((), (), s32[]{:S(2)}) async-start(), calls=%async_computation.25 | async-start | bytes 589824
  1083.0 250.2 %all-reduce.12.cloned.1.call-start = ((), (), s32[]{:S(2)}) async-start(), calls=%async_computation.26 | async-start | bytes 8388608 | tf_op jit(solution)/shard_map/psum | solution.py:192
  1142.4 244.7 %reduce-scatter.20.cloned.1.call-start = ((), (), s32[]{:S(2)}) async-start(), calls=%async_computation.22 | async-start | bytes 4718592 | tf_op jit(solution)/shard_map/reduce_scatter | solution.py:309
  1151.1 291.1 %reduce-scatter.18.cloned.1.call-start = ((), (), s32[]{:S(2)}) async-start(), calls=%async_computation.21 | async-start | bytes 4718592 | tf_op jit(solution)/shard_map/reduce_scatter | solution.py:308
  1157.2 324.6 %reduce-scatter.16.cloned.1.call-start = ((), (), s32[]{:S(2)}) async-start(), calls=%async_computation.20 | async-start | bytes 1179648 | tf_op jit(solution)/shard_map/reduce_scatter | solution.py:305
  1162.1 369.6 %reduce-scatter.14.cloned.1.call-start = ((), (), s32[]{:S(2)}) async-start(), calls=%async_computation.19 | async-start | bytes 3538944 | tf_op jit(solution)/shard_map/reduce_scatter | solution.py:304
  1189.0 147.7 %copy-start.52 = (f32[1024]{0:T(1024)S(1)}, f32[1024]{0:T(1024)}, u32[]{:S(2)}) copy-start(f32[1024]{0:T(1024)} %get-tuple-element.292) | copy-start | bytes 12292
  1352.6 179.1 %copy-start.1 = (bf16[1,1024,1024]{2,1,0:T(8,128)(2,1)S(1)}, bf16[1,1024,1024]{2,1,0:T(8,128)(2,1)}, u32[]{:S(2)}) copy-start(bf16[1,1024,1024]{2,1,0:T(8,128)(2,1)} %param.30) | copy-start | bytes 6291460
  (54 other events, 612.7 us)
Sparse Core Ops, SparseCore 0:
  10.5 28.4 all-gather.9
  44.3 38.9 all-gather.17
  85.7 35.1 all-gather.15
  201.4 86.1 all-reduce.7
  311.7 59.7 all-gather.11
  440.7 60.1 all-gather.13
  810.2 83.0 all-reduce.9
  1065.1 34.2 reduce-scatter.11
  1102.3 35.1 reduce-scatter.9
  1141.0 34.1 reduce-scatter.21
  1178.2 155.0 all-reduce.11
  1337.0 50.0 reduce-scatter.19
  1391.0 51.1 reduce-scatter.17
  1445.8 35.9 reduce-scatter.15
  1485.6 46.0 reduce-scatter.13
where the time goes:
time: 1540 us
  waiting for transfers between devices  702 us (46%)
  matrix products  287 us (19%)
  blocking collectives  242 us (16%)
  local copies, waits for them, and re-layouts  155 us (10%)
  other arithmetic  116 us (8%)
  starting transfers between devices  19.9 us (1%)
  between operations  16.5 us (1%)
    psum x1, waiting for transfers between devices, local(): mixed = lax.psum(mixed_part.astype(jnp.bfloat16), 'tp').astype(jnp.float32)  144 us
    all_gather x1, blocking collectives, local(): lax.all_gather(mix_weight, ('shard', 'ctx'), axis=0, tiled=True)  86.6 us
    psum x1, waiting for transfers between devices, local(): lax.psum((normed2_part + expert_tok_grad).astype(jnp.bfloat16), 'tp')  83.1 us
    all_to_all x1, blocking collectives, local(): lax.all_to_all(pack_rows(expert_grad), ('shard', 'ctx'), split_axis=0, co...  76.7 us
    all_to_all x1, waiting for transfers between devices, local(): lax.all_to_all(pack_rows(normed2_low), ('shard', 'ctx'), split_axis=0, co...  66.5 us
    all_to_all x1, waiting for transfers between devices, local(): lax.all_to_all(unfold_rows(expert_in_grad).astype(jnp.bfloat16), ('shard'...  62.3 us
    psum x1, waiting for transfers between devices, local(): lax.psum(branch_part.astype(jnp.bfloat16), 'tp').astype(jnp.float32)  59.8 us
    reduce_scatter x1, waiting for transfers between devices, local(): lax.psum_scatter(up_grad, ('shard', 'ctx'), scatter_dimension=0, tiled=True)  55.1 us
  transfers between devices with their start and end apart: 19, of which 15 were waited for; matrix products, arithmetic and copies ran while one was open for 13% of the time, Pallas kernels for 0%

commit v1 on v0

--- a/solution.py
+++ b/solution.py
@@ -223,8 +223,9 @@
         tiled=True,
     ).astype(jnp.float32)
     expert_tok_grad = sent_back.reshape(-1, model_width)[full_index] * live_rows
+    post_plane = lambda xx: jnp.sum(lax.all_gather(xx, axis_name="tp"), axis=0)
     normed2_grad, branch_dots = (
-        lax.psum((normed2_part + expert_tok_grad).astype(jnp.bfloat16), "tp").astype(jnp.float32),
+        post_plane((normed2_part + expert_tok_grad).astype(jnp.bfloat16)).astype(jnp.float32),
         lax.psum(dots_part.astype(jnp.bfloat16), "tp").astype(jnp.float32),
     )
     logit_grad = mixing * (branch_dots - jnp.sum(mixing * branch_dots, axis=-1, keepdims=True))

time: 1540 us -> 1610 us (1.045)
  waiting for transfers between devices: 702 us -> 764 us
    all_gather x0 -> x1, waiting for transfers between devices: none -> 147 us  [local(): post_plane = lambda xx: jnp.sum(lax.all_gather(xx, axis_name='tp'), axis=0)]
    psum x1 -> x0, waiting for transfers between devices: 83.1 us -> none  [local(): lax.psum((normed2_part + expert_tok_grad).astype(jnp.bfloat16), 'tp')]
where the time goes in v1:
time: 1610 us
  waiting for transfers between devices  764 us (47%)
  matrix products  286 us (18%)
  blocking collectives  242 us (15%)
  local copies, waits for them, and re-layouts  155 us (10%)
  other arithmetic  124 us (8%)
  starting transfers between devices  19.7 us (1%)
  between operations  16.5 us (1%)
    all_gather x1, waiting for transfers between devices, local(): post_plane = lambda xx: jnp.sum(lax.all_gather(xx, axis_name='tp'), axis=0)  147 us
    psum x1, waiting for transfers between devices, local(): mixed = lax.psum(mixed_part.astype(jnp.bfloat16), 'tp').astype(jnp.float32)  144 us
    all_gather x1, blocking collectives, local(): lax.all_gather(mix_weight, ('shard', 'ctx'), axis=0, tiled=True)  86.6 us
    all_to_all x1, blocking collectives, local(): lax.all_to_all(pack_rows(expert_grad), ('shard', 'ctx'), split_axis=0, co...  76.7 us
    all_to_all x1, waiting for transfers between devices, local(): lax.all_to_all(pack_rows(normed2_low), ('shard', 'ctx'), split_axis=0, co...  66.5 us
    all_to_all x1, waiting for transfers between devices, local(): lax.all_to_all(unfold_rows(expert_in_grad).astype(jnp.bfloat16), ('shard'...  62.3 us
    psum x1, waiting for transfers between devices, local(): lax.psum(branch_part.astype(jnp.bfloat16), 'tp').astype(jnp.float32)  59.9 us
    reduce_scatter x1, waiting for transfers between devices, local(): lax.psum_scatter(up_grad, ('shard', 'ctx'), scatter_dimension=0, tiled=True)  55.1 us
  transfers between devices with their start and end apart: 19, of which 15 were waited for; matrix products, arithmetic and copies ran while one was open for 13% of the time, Pallas kernels for 0%

profile of v1, /device:TPU:0, one launch (start us, length us, event | category | flops | bytes accessed | tf_op | source)
XLA Modules:
  0.0 1608.7 jit_solution(11637996669362147959)
XLA Ops:
  9.2 15.0 all-gather.3
  28.5 10.5 all-gather.12.cloned.1.call-done
  45.0 24.8 %all_gather.37 = bf16[256,1024]{1,0:T(8,128)(2,1)S(1)} all-gather(bf16[256,128]{1,0:T(8,128)(2,1)S(1)} %copy-done.32), channel_id=1, replica_groups=mesh['shard'=2,'ctx'=4,'tp'=4] {'shard','ctx'}, dimensions={1}, use_global_device_ids=true | all-gather | bytes 589824 | tf_op jit(solution)/shard_map/all_gather | solution.py:62
  69.8 13.2 all-gather.20.cloned.1.call-done
  90.9 29.6 %all-gather.18.cloned.1.call-done = bf16[4096,1,256]{0,2,1:T(8,128)(2,1)} async-done(((bf16[1024,1,256]{0,2,1:T(8,128)(2,1)}), bf16[4096,1,256]{0,2,1:T(8,128)(2,1)}) %all-gather.18.cloned.1.call-update) | async-done | bytes 2097168 | tf_op jit(solution)/shard_map/all_gather | solution.py:79
  128.6 67.9 %while.30 = (s32[]{:T(128)}, f32[4,1024]{1,0:T(4,128)S(1)}, f32[4,1024]{1,0:T(4,128)S(1)}, f32[4,1024,64]{1,2,0:T(8,128)}, s32[4,1024]{1,0:T(4,128)S(1)}, /*inde...) while((s32[]{:T(128)}, f32[4,1024]{1,0:T(4,128)S(1)}, ...), condition=%wide.region_5.6_spmd.clone, body=%wide.region_2.5_spmd.clone.sunk | while | flops 1131173888 | bytes 66869456 | solution.py:117
  212.9 14.5 all-gather.4
  227.4 59.9 %all-reduce.7.cloned.1.call-done = bf16[1024,1024]{1,0:T(8,128)(2,1)} async-done(((bf16[1024,1024]{1,0:T(8,128)(2,1)}), bf16[1024,1024]{1,0:T(8,128)(2,1)}) %all-reduce.7.cloned.1.call-update) | async-done | bytes 2097168 | tf_op jit(solution)/shard_map/psum | solution.py:124
  294.5 9.8 scatter_custom_fusion.1
  321.9 66.5 %all-to-all-done.1 = bf16[8,384,1024]{2,1,0:T(8,128)(2,1)} async-done(((bf16[8,384,1024]{2,1,0:T(8,128)(2,1)}), bf16[8,384,1024]{2,1,0:T(8,128)(2,1)}, u32[]{:S(2)}, u32[]{:S(2)}) %all-to-all-start.1) | async-done | bytes 6291488 | tf_op jit(solution)/shard_map/all_to_all | solution.py:157
  388.4 10.2 gather_fusion
  410.3 14.8 scatter_custom_fusion.2
  438.8 86.6 %all_gather.39 = bf16[1024,2]{0,1:T(2,128)(2,1)S(1)} all-gather(bf16[128,2]{0,1:T(2,128)(2,1)S(1)} %copy-done.54), channel_id=1, replica_groups=mesh['shard'=2,'ctx'=4,'tp'=4] {'shard','ctx'}, dimensions={0}, use_global_device_ids=true | all-gather | bytes 4608 | tf_op jit(solution)/shard_map/all_gather | solution.py:64
  543.2 10.9 gather_fusion.2
  554.1 9.6 fusion.91
  563.7 10.0 psum.30
  573.8 10.1 scatter_custom_fusion.3
  583.8 76.7 %all_to_all.29 = bf16[8,384,1024]{2,1,0:T(8,128)(2,1)} all-to-all(bf16[8,384,1024]{2,1,0:T(8,128)(2,1)} %bitcast.323), channel_id=1, replica_groups=mesh['shard'=2,'ctx'=4,'tp'=4] {'shard','ctx'}, dimensions={0} | all-to-all | bytes 12582912 | tf_op jit(solution)/shard_map/all_to_all | solution.py:206
  660.5 10.2 gather_fusion.3
  684.4 14.3 scatter_custom_fusion.4
  720.5 62.3 %all-to-all-done.4 = bf16[8,384,1024]{2,1,0:T(8,128)(2,1)} async-done(((bf16[8,384,1024]{2,1,0:T(8,128)(2,1)}), bf16[8,384,1024]{2,1,0:T(8,128)(2,1)}, u32[]{:S(2)}, u32[]{:S(2)}) %all-to-all-start.4) | async-done | bytes 6291488 | tf_op jit(solution)/shard_map/all_to_all | solution.py:218
  791.7 11.0 gather_fusion.4
  810.0 146.6 %all-gather.22.cloned.1.call-done = bf16[4096,1024]{1,0:T(8,128)(2,1)} async-done(((bf16[1024,1024]{1,0:T(8,128)(2,1)}), bf16[4096,1024]{1,0:T(8,128)(2,1)}) %all-gather.22.cloned.1.call-update) | async-done | bytes 8388624 | tf_op jit(solution)/shard_map/all_gather | solution.py:226
  977.9 144.0 %while.31 = (s32[]{:T(128)}, f32[1024,4,64]{0,2,1:T(8,128)S(1)}, f32[4,1024,4,64]{1,3,2,0:T(8,128)}, bf16[4,1024,4,64]{1,3,2,0:T(8,128)(2,1)}, bf16[4,1024,4,64]...) while((s32[]{:T(128)}, f32[1024,4,64]{0,2,1:T(8,128)S(1)}, ...), condition=%wide.region_30.31_spmd.clone, body=%wide.region_29.30_spmd.clone.sunk | while | flops 2728921088 | bytes 86579392 | solution.py:278
  1156.1 13.2 reduce-scatter.12.cloned.1.call-done
  1169.4 38.2 %reduce-scatter.10.cloned.1.call-done = bf16[1024,256]{1,0:T(8,128)(2,1)} async-done(((bf16[4096,256]{1,0:T(8,128)(2,1)}), bf16[1024,256]{1,0:T(8,128)(2,1)}) %reduce-scatter.10.cloned.1.call-update) | async-done | bytes 524304 | tf_op jit(solution)/shard_map/reduce_scatter | solution.py:286
  1259.0 144.2 %all-reduce.9.cloned.1.call-done = (bf16[1024,1024]{1,0:T(8,128)(2,1)}, bf16[1024,1024]{1,0:T(8,128)(2,1)}) async-done(((bf16[1024,1024]{1,0:T(8,128)(2,1)}, bf16[1024,1024]{1,0:T(8,128)(2,1)}), (bf16[1024,1024]{1,0:T(8,128)(2,1)}, bf16[1024,1024]{1,0:T(8,128)(2,1)})) %all-reduce.9.cloned.1.call-update) | async-done | bytes 4194320 | tf_op jit(solution)/shard_map/psum | solution.py:192
  1406.8 14.7 all-reduce.2
  1429.8 27.3 %reduce-scatter.20.cloned.1.call-done = f32[1024,128]{1,0:T(8,128)} async-done(((f32[1024,1024]{1,0:T(8,128)}), f32[1024,128]{1,0:T(8,128)}) %reduce-scatter.20.cloned.1.call-update) | async-done | bytes 524304 | tf_op jit(solution)/shard_map/reduce_scatter | solution.py:310
  1457.1 55.1 %reduce-scatter.18.cloned.1.call-done = f32[128,1024]{1,0:T(8,128)} async-done(((f32[1024,1024]{1,0:T(8,128)}), f32[128,1024]{1,0:T(8,128)}) %reduce-scatter.18.cloned.1.call-update) | async-done | bytes 524304 | tf_op jit(solution)/shard_map/reduce_scatter | solution.py:309
  1512.2 39.6 %reduce-scatter.16.cloned.1.call-done = f32[256,128]{1,0:T(8,128)} async-done(((f32[256,1024]{1,0:T(8,128)}), f32[256,128]{1,0:T(8,128)}) %reduce-scatter.16.cloned.1.call-update) | async-done | bytes 131088 | tf_op jit(solution)/shard_map/reduce_scatter | solution.py:306
  1551.8 49.9 %reduce-scatter.14.cloned.1.call-done = f32[128,3,256]{2,0,1:T(8,128)} async-done(((f32[1024,3,256]{2,0,1:T(8,128)}), f32[128,3,256]{2,0,1:T(8,128)}) %reduce-scatter.14.cloned.1.call-update) | async-done | bytes 393232 | tf_op jit(solution)/shard_map/reduce_scatter | solution.py:305
  (334 shorter events, 492.6 us)
Async XLA Ops:
  7.2 398.5 %copy-start = (bf16[1,1024,1024]{2,1,0:T(8,128)(2,1)S(1)}, bf16[1,1024,1024]{2,1,0:T(8,128)(2,1)}, u32[]{:S(2)}) copy-start(bf16[1,1024,1024]{2,1,0:T(8,128)(2,1)} %param.30) | copy-start | bytes 6291460
  7.2 31.8 %all-gather.12.cloned.1.call-start = ((), (), s32[]{:S(2)}) async-start(), calls=%async_computation.12 | async-start | bytes 1769472 | tf_op jit(solution)/shard_map/all_gather | solution.py:61
  9.1 73.8 %all-gather.20.cloned.1.call-start = ((), (), s32[]{:S(2)}) async-start(), calls=%async_computation.23 | async-start | bytes 2621440 | tf_op jit(solution)/shard_map/all_gather | solution.py:80
  44.2 76.4 %all-gather.18.cloned.1.call-start = ((), (), s32[]{:S(2)}) async-start(), calls=%async_computation.22 | async-start | bytes 2621440 | tf_op jit(solution)/shard_map/all_gather | solution.py:79
  44.9 242.4 %all-reduce.7.cloned.1.call-start = ((), (), s32[]{:S(2)}) async-start(), calls=%async_computation.13 | async-start | bytes 4194304 | tf_op jit(solution)/shard_map/psum | solution.py:124
  69.8 128.3 %copy-start.14 = (bf16[256,1024]{1,0:T(8,128)(2,1)}, bf16[256,1024]{1,0:T(8,128)(2,1)S(1)}, u32[]{:S(2)}) copy-start(bf16[256,1024]{1,0:T(8,128)(2,1)S(1)} %all_gather.37) | copy-start | bytes 1572868
  196.5 93.8 %copy-start.23 = (f32[4,1024]{1,0:T(4,128)}, f32[4,1024]{1,0:T(4,128)S(1)}, u32[]{:S(2)}) copy-start(f32[4,1024]{1,0:T(4,128)S(1)} %get-tuple-element.138) | copy-start | bytes 49156
  196.5 93.8 %copy-start.25 = (f32[4,1024]{1,0:T(4,128)}, f32[4,1024]{1,0:T(4,128)S(1)}, u32[]{:S(2)}) copy-start(f32[4,1024]{1,0:T(4,128)S(1)} %get-tuple-element.136) | copy-start | bytes 49156
  196.5 93.8 %copy-start.27 = (s32[4,1024]{1,0:T(4,128)}, s32[4,1024]{1,0:T(4,128)S(1)}, u32[]{:S(2)}) copy-start(s32[4,1024]{1,0:T(4,128)S(1)} %get-tuple-element.680) | copy-start | bytes 49156
  209.6 94.7 %all-to-all-start = ((s32[8,1,384]{2,1,0:T(1,128)}), s32[8,1,384]{2,1,0:T(1,128)S(1)}, u32[]{:S(2)}, u32[]{:S(2)}) async-start(s32[8,1,384]{2,1,0:T(1,128)} %bitcast.19), calls=%async_computation | async-start | bytes 24576 | tf_op jit(solution)/shard_map/all_to_all | solution.py:160
  227.4 64.3 %copy-start.44 = (f32[8,1,128]{2,1,0:T(1,128)}, f32[8,1,128]{2,1,0:T(1,128)S(1)}, u32[]{:S(2)}) copy-start(f32[8,1,128]{2,1,0:T(1,128)S(1)} %convert_element_type.208) | copy-start | bytes 12292
  304.3 84.1 %all-to-all-start.1 = ((bf16[8,384,1024]{2,1,0:T(8,128)(2,1)}), bf16[8,384,1024]{2,1,0:T(8,128)(2,1)}, u32[]{:S(2)}, u32[]{:S(2)}) async-start(bf16[8,384,1024]{2,1,0:T(8,128)(2,1)} %bitcast.322), calls=%async_computation.1 | async-start | bytes 12582912 | tf_op jit(solution)/shard_map/all_to_all | solution.py:157
  309.0 218.7 %all-gather.14.cloned.1.call-start = ((), (), s32[]{:S(2)}) async-start(), calls=%async_computation.14 | async-start | bytes 2359296 | tf_op jit(solution)/shard_map/all_gather | solution.py:65
  433.3 101.0 %all-to-all-start.2 = ((bf16[8,384,1024]{2,1,0:T(8,128)(2,1)}), bf16[8,384,1024]{2,1,0:T(8,128)(2,1)}, u32[]{:S(2)}, u32[]{:S(2)}) async-start(bf16[8,384,1024]{2,1,0:T(8,128)(2,1)} %bitcast.324), calls=%async_computation.2 | async-start | bytes 12582912 | tf_op jit(solution)/shard_map/all_to_all | solution.py:183
  438.2 115.8 %all-gather.16.cloned.1.call-start = ((), (), s32[]{:S(2)}) async-start(), calls=%async_computation.15 | async-start | bytes 2359296 | tf_op jit(solution)/shard_map/all_gather | solution.py:66
  525.4 445.6 %copy-start.30 = (f32[1024]{0:T(1024)}, f32[1024]{0:T(1024)S(1)}, u32[]{:S(2)}) copy-start(f32[1024]{0:T(1024)S(1)} %fusion.129) | copy-start | bytes 12292
  573.7 390.5 %copy-start.37 = (bf16[1024,2]{0,1:T(2,128)(2,1)}, bf16[1024,2]{0,1:T(2,128)(2,1)S(1)}, u32[]{:S(2)}) copy-start(bf16[1024,2]{0,1:T(2,128)(2,1)S(1)} %psum.30) | copy-start | bytes 12292
  573.7 390.5 %copy-start.28 = (f32[1024,2]{0,1:T(2,128)}, f32[1024,2]{0,1:T(2,128)S(1)}, u32[]{:S(2)}) copy-start(f32[1024,2]{0,1:T(2,128)S(1)} %get-tuple-element.357) | copy-start | bytes 24580
  573.7 390.5 %copy-start.50 = (f32[1024]{0:T(1024)}, f32[1024]{0:T(1024)S(1)}, u32[]{:S(2)}) copy-start(f32[1024]{0:T(1024)S(1)} %get-tuple-element.356) | copy-start | bytes 12292
  573.8 397.2 %copy-start.48 = (f32[1024,1]{0,1:T(1,128)}, f32[1024,1]{0,1:T(1,128)S(1)}, u32[]{:S(2)}) copy-start(f32[1024,1]{0,1:T(1,128)S(1)} %get-tuple-element.365) | copy-start | bytes 12292
  706.9 75.9 %all-to-all-start.4 = ((bf16[8,384,1024]{2,1,0:T(8,128)(2,1)}), bf16[8,384,1024]{2,1,0:T(8,128)(2,1)}, u32[]{:S(2)}, u32[]{:S(2)}) async-start(bf16[8,384,1024]{2,1,0:T(8,128)(2,1)} %bitcast.325), calls=%async_computation.4 | async-start | bytes 12582912 | tf_op jit(solution)/shard_map/all_to_all | solution.py:218
  711.8 244.7 %all-gather.22.cloned.1.call-start = ((), (), s32[]{:S(2)}) async-start(), calls=%async_computation.24 | async-start | bytes 10485760 | tf_op jit(solution)/shard_map/all_gather | solution.py:226
  809.9 359.5 %reduce-scatter.12.cloned.1.call-start = ((), (), s32[]{:S(2)}) async-start(), calls=%async_computation.17 | async-start | bytes 2621440 | tf_op jit(solution)/shard_map/reduce_scatter | solution.py:289
  1135.8 71.7 %reduce-scatter.10.cloned.1.call-start = ((), (), s32[]{:S(2)}) async-start(), calls=%async_computation.16 | async-start | bytes 2621440 | tf_op jit(solution)/shard_map/reduce_scatter | solution.py:286
  1150.7 94.5 %reduce-scatter.22.cloned.1.call-start = ((), (), s32[]{:S(2)}) async-start(), calls=%async_computation.25 | async-start | bytes 589824
  1153.9 249.3 %all-reduce.9.cloned.1.call-start = ((), (), s32[]{:S(2)}) async-start(), calls=%async_computation.26 | async-start | bytes 8388608 | tf_op jit(solution)/shard_map/psum | solution.py:192
  1212.4 244.7 %reduce-scatter.20.cloned.1.call-start = ((), (), s32[]{:S(2)}) async-start(), calls=%async_computation.21 | async-start | bytes 4718592 | tf_op jit(solution)/shard_map/reduce_scatter | solution.py:310
  1221.1 291.1 %reduce-scatter.18.cloned.1.call-start = ((), (), s32[]{:S(2)}) async-start(), calls=%async_computation.20 | async-start | bytes 4718592 | tf_op jit(solution)/shard_map/reduce_scatter | solution.py:309
  1227.2 324.6 %reduce-scatter.16.cloned.1.call-start = ((), (), s32[]{:S(2)}) async-start(), calls=%async_computation.19 | async-start | bytes 1179648 | tf_op jit(solution)/shard_map/reduce_scatter | solution.py:306
  1232.1 369.5 %reduce-scatter.14.cloned.1.call-start = ((), (), s32[]{:S(2)}) async-start(), calls=%async_computation.18 | async-start | bytes 3538944 | tf_op jit(solution)/shard_map/reduce_scatter | solution.py:305
  1259.0 147.7 %copy-start.52 = (f32[1024]{0:T(1024)S(1)}, f32[1024]{0:T(1024)}, u32[]{:S(2)}) copy-start(f32[1024]{0:T(1024)} %get-tuple-element.292) | copy-start | bytes 12292
  1422.6 179.1 %copy-start.1 = (bf16[1,1024,1024]{2,1,0:T(8,128)(2,1)S(1)}, bf16[1,1024,1024]{2,1,0:T(8,128)(2,1)}, u32[]{:S(2)}) copy-start(bf16[1,1024,1024]{2,1,0:T(8,128)(2,1)} %param.30) | copy-start | bytes 6291460
  (54 other events, 307.2 us)
Sparse Core Ops, SparseCore 0:
  10.5 28.4 all-gather.11
  44.3 38.6 all-gather.19
  85.4 35.1 all-gather.17
  201.1 86.1 all-reduce.6
  311.4 59.7 all-gather.13
  440.6 60.1 all-gather.15
  810.0 146.5 all-gather.21
  1135.9 33.3 reduce-scatter.11
  1172.3 35.1 reduce-scatter.9
  1211.1 34.1 reduce-scatter.21
  1248.2 154.9 all-reduce.8
  1407.0 50.0 reduce-scatter.19
  1461.0 51.1 reduce-scatter.17
  1515.8 35.9 reduce-scatter.15
  1555.6 46.0 reduce-scatter.13
